TPU v7x, 256 devices: a whole 4x4x8 slice. The times are simulated.
256 devices in a mesh: cache: 32 (over x, z), owner: 8 (over y, core).
Axes of the slice: x: 4, y: 4, z: 8, core: 2. Of those that a mesh axis runs over, the one named last changes fastest.
Arguments:
- cache: bfloat16 [32, 4, 128, 256], P('cache'), may hold values from -2.5 to 2.5
- backing: bfloat16 [32, 64, 128, 256], P('cache', 'owner'), may hold values from -2.5 to 2.5
- resident: int32 [32, 4], P('cache'), may hold values from 0 to 63, as said below
- promote: int32 [32, 2], P('cache'), may hold values from 0 to 63, as said below
- victim: int32 [32, 2], P('cache'), may hold values from 0 to 3, as said below
- lookups: int32 [2, 32768, 32, 8], P(None, 'owner', 'cache'), may hold values from 0 to 511
- route: int32 [2, 8, 4096], P(None, 'owner'), may hold values from 0 to 4095, each once within a row
- dcn_down: bfloat16 [8192, 128], P('cache'), may hold values from -0.0625 to 0.0625
- dcn_up: bfloat16 [128, 8192], P(None, 'cache'), may hold values from -0.5 to 0.5
- dcn_bias: float32 [8192], replicated, may hold values from -5 to 5
- mlp_in: bfloat16 [8192, 1024], P('cache'), may hold values from -0.0625 to 0.0625
- mlp_bias: float32 [1024], replicated, may hold values from -3 to 3
- mlp_out: float32 [1024], replicated, may hold values from -0.1875 to 0.1875
- out_bias: float32 [1], replicated, may hold values from -4 to 4
Outputs:
- scores: float32 [2, 8, 4096], P(None, 'owner', 'cache')
- new_cache: bfloat16 [32, 4, 128, 256], P('cache')
- new_backing: bfloat16 [32, 64, 128, 256], P('cache', 'owner')
Inputs may be any that keep to these rules, and one draw needn't show every extreme that they name: `resident`: for each feature, 4 distinct backing blocks. `promote`: for each feature, 2 distinct backing blocks, none of them in that feature's resident; block k belongs to owner k // 8. `victim`: for each feature, 2 distinct slots. `route`: each batch and owner group holds every request index once.
All inputs are finite; a program needn't handle non-finite values.
Results may differ from a plain program's by a relative error of at most 0.004.
Values may be sent and summed in bfloat16 or wider, within the bound.
No kernel may reach another device: no remote copies, remote signals or barrier semaphores. Data moves between devices by JAX's collectives and lax.ppermute only.
A program may use at most 128 MiB of HBM per device.

v0:
```python
import jax
import jax.numpy as jnp
from jax import lax
from jax.sharding import PartitionSpec as P


def copy_for_each(x, axis):
    size = lax.axis_size(axis)
    return lax.all_to_all(jnp.broadcast_to(x[None], (size, *x.shape)), axis, 0, 0, tiled=True)


def in_order(blocks, dim):
    lengths = list(blocks.shape[1:])
    lengths[dim] *= blocks.shape[0]
    return jnp.moveaxis(blocks, 0, dim).reshape(lengths)


def gathered_copies(x, axis, dim):
    blocks = copy_for_each(x, axis)
    return in_order(blocks, dim)


def take_rows(table, wanted):
    return jax.vmap(lambda rows, chosen: rows[chosen])(table, wanted)


def pool_batch(requests, order, table):
    requests = requests[order]
    count = requests.shape[0]
    step = min(512, count)
    codes = jnp.arange(table.shape[1], dtype=jnp.int32)

    def one_block(lookup_block):
        counts = jnp.sum((lookup_block[..., None] == codes).astype(jnp.bfloat16), axis=2)
        return jnp.einsum("rfk,fke->rfe", counts, table, preferred_element_type=jnp.float32).astype(
            jnp.bfloat16
        )

    blocks = requests.reshape((count // step, step) + requests.shape[1:])
    pooled = lax.map(one_block, blocks)
    return pooled.reshape((count,) + pooled.shape[2:])


def on_device(
    cache,
    backing,
    resident,
    promote,
    victim,
    lookups,
    route,
    dcn_down,
    dcn_up,
    dcn_bias,
    mlp_in,
    mlp_bias,
    mlp_out,
    out_bias,
):
    held = cache.shape[0]
    slots = cache.shape[1]
    block = cache.shape[2]
    width = cache.shape[3]
    own_blocks = backing.shape[1]
    promoted_count = promote.shape[1]
    owner_here = lax.axis_index("owner")
    local_index = promote - owner_here * own_blocks
    owned_here = (local_index >= 0) & (local_index < own_blocks)
    clamped = jnp.clip(local_index, 0, own_blocks - 1)
    fetched = take_rows(backing, clamped)
    outgoing = jnp.where(owned_here[:, :, None, None], fetched, jnp.zeros_like(fetched))
    arrived = gathered_copies(outgoing, "owner", 0)
    owners = arrived.shape[0] // held
    arrived = arrived.reshape(owners, held, promoted_count, block, width)
    source = promote // own_blocks
    picked = source[None] == jnp.arange(owners, dtype=jnp.int32)[:, None, None]
    promoted = jnp.sum(jnp.where(picked[..., None, None], arrived, jnp.zeros_like(arrived)), axis=0)
    evicted = take_rows(cache, victim)
    leaving = take_rows(resident, victim) - owner_here * own_blocks
    slot_numbers = jnp.arange(slots, dtype=jnp.int32)
    block_numbers = jnp.arange(own_blocks, dtype=jnp.int32)
    new_cache = cache
    new_backing = backing
    for column in range(promoted_count):
        slot_hit = victim[:, column][:, None] == slot_numbers[None, :]
        new_cache = jnp.where(slot_hit[:, :, None, None], promoted[:, column][:, None], new_cache)
        block_hit = leaving[:, column][:, None] == block_numbers[None, :]
        new_backing = jnp.where(
            block_hit[:, :, None, None], evicted[:, column][:, None], new_backing
        )
    table = new_cache.reshape(held, slots * block, width)
    batches = lookups.shape[0]
    received = []
    for batch_turn in range(batches):
        pooled = pool_batch(lookups[batch_turn], route[batch_turn, 0], table)
        received.append(lax.all_to_all(pooled, "cache", split_axis=0, concat_axis=1, tiled=True))
    arrived_rows = jnp.stack(received)
    per_batch = arrived_rows.shape[1]
    features = arrived_rows.reshape(batches * per_batch, -1)
    columns = features
    low = jnp.dot(
        columns,
        lax.all_gather(dcn_down, "cache", axis=0, tiled=True),
        preferred_element_type=jnp.float32,
    ).astype(jnp.bfloat16)
    gate = (
        jnp.dot(
            low,
            lax.all_gather(dcn_up, "cache", axis=1, tiled=True),
            preferred_element_type=jnp.float32,
        )
        + dcn_bias
    )
    crossed = (features * gate + features).astype(jnp.bfloat16)
    columns = crossed
    before = jnp.dot(
        columns,
        lax.all_gather(mlp_in, "cache", axis=0, tiled=True),
        preferred_element_type=jnp.float32,
    )
    hidden = jnp.maximum(before + mlp_bias, 0.0)
    scores = jnp.sum(hidden * mlp_out, axis=-1) + out_bias[0]
    return (scores.reshape(batches, 1, per_batch), new_cache, new_backing)


def solution(mesh):
    in_specs = (
        P("cache", None, None, None),
        P("cache", "owner", None, None),
        P("cache", None),
        P("cache", None),
        P("cache", None),
        P(None, "owner", "cache", None),
        P(None, "owner", None),
        P("cache", None),
        P(None, "cache"),
        P(),
        P("cache", None),
        P(),
        P(),
        P(),
    )
    out_specs = (
        P(None, "owner", "cache"),
        P("cache", None, None, None),
        P("cache", "owner", None, None),
    )
    return jax.shard_map(
        on_device, mesh=mesh, in_specs=in_specs, out_specs=out_specs, check_vma=False
    )
```

profile of v0, /device:TPU:1, one launch (start us, length us, event | category | flops | bytes accessed | tf_op | source)
XLA Modules:
  0.0 363.3 jit_solution(7484960167387886002)
XLA Ops:
  10.4 1.6 gather_fusion.2
  12.8 1.1 broadcast_in_dim.137
  13.9 6.7 %all-to-all-start = ((bf16[8,1,2,128,256]{4,3,2,1,0:T(8,128)(2,1)}), bf16[8,1,2,128,256]{4,3,2,1,0:T(8,128)(2,1)S(1)}, u32[]{:S(2)}, u32[]{:S(2)}) async-start(bf16[8,1,2,128,256]{4,3,2,1,0:T(8,128)(2,1)} %broadcast_in_dim.137), calls=%async_computation | async-start | bytes 2097152 | tf_op jit(solution)/shard_map/all_to_all | solution.py:9
  21.2 14.1 %gather_fusion = s32[4096,8]{1,0:T(8,128)} fusion(s32[4096,8]{1,0:T(8,128)S(1)} %bitcast.111, s32[4096]{0:T(1024)S(1)} %broadcast_clamp_fusion.1), kind=kCustom, calls=%fused_computation | custom fusion | bytes 278528 | tf_op jit(solution)/shard_map/gather | solution.py:28
  35.4 2.8 copy.64
  38.8 14.1 %gather_fusion.1 = s32[4096,8]{1,0:T(8,128)} fusion(s32[4096,8]{1,0:T(8,128)S(1)} %bitcast.110, s32[4096]{0:T(1024)S(1)} %broadcast_clamp_fusion), kind=kCustom, calls=%fused_computation.1 | custom fusion | bytes 278528 | tf_op jit(solution)/shard_map/gather | solution.py:28
  52.9 2.2 copy.67
  55.8 1.3 iota_compare_fusion.5
  57.6 35.3 %while.26 = (s32[]{:T(128)}, bf16[8,512,1,256]{3,1,2,0:T(8,128)(2,1)S(1)}, s32[8,512,1,8]{1,3,2,0:T(8,128)}, bf16[1,512,256]{2,1,0:T(8,128)(2,1)S(1)}, s32[]{:T(128)}) while((s32[]{:T(128)}, bf16[8,512,1,256]{3,1,2,0:T(8,128)(2,1)S(1)}, s32[8,512,1,8]{1,3,2,0:T(8,128)}, bf16[1,512,256]{2,1,0:T(8,128)(2,1)S(1)}, s32[]{:T(128)}) %tuple.90), condition=%wide.region_3.4_spmd.clone, body=%wide.region_1.3_spmd.clone.sunk | while | flops 140378112 | bytes 1654853 | solution.py:40
  58.4 3.2 fusion.41
  62.8 3.2 fusion.41
  67.2 3.2 fusion.41
  71.7 3.2 fusion.41
  76.1 3.2 fusion.41
  80.5 3.2 fusion.41
  84.9 3.2 fusion.41
  89.3 3.2 fusion.41
  93.4 2.9 reduce.17
  96.3 4.0 %reshape.321 = bf16[32,2,16384]{2,1,0:T(2,128)(2,1)} reshape(bf16[4096,256]{1,0:T(8,128)(2,1)} %reduce.17) | data formatting | bytes 4194304
  100.3 10.3 %all-to-all-start.1 = ((bf16[32,2,16384]{2,1,0:T(2,128)(2,1)}), bf16[32,2,16384]{2,1,0:T(2,128)(2,1)S(1)}, u32[]{:S(2)}, u32[]{:S(2)}) async-start(bf16[32,2,16384]{2,1,0:T(2,128)(2,1)} %reshape.321), calls=%async_computation.1 | async-start | bytes 4194304 | tf_op jit(solution)/shard_map/all_to_all | solution.py:96
  110.6 1.5 broadcast.187.clone
  112.1 35.1 %while.27 = (s32[]{:T(128)}, bf16[8,512,1,256]{3,1,2,0:T(8,128)(2,1)}, s32[8,512,1,8]{1,3,2,0:T(8,128)S(1)}, bf16[1,512,256]{2,1,0:T(8,128)(2,1)S(1)}, s32[]{:T(128)}) while((s32[]{:T(128)}, bf16[8,512,1,256]{3,1,2,0:T(8,128)(2,1)}, s32[8,512,1,8]{1,3,2,0:T(8,128)S(1)}, bf16[1,512,256]{2,1,0:T(8,128)(2,1)S(1)}, s32[]{:T(128)}) %tuple.91), condition=%wide.region_6.7_spmd.clone, body=%wide.region_4.6_spmd.clone.sunk | while | flops 140378112 | bytes 1655361 | solution.py:40
  112.2 3.2 fusion.45
  115.5 1.0 fusion.46
  116.6 3.2 fusion.45
  119.9 1.0 fusion.46
  121.0 3.2 fusion.45
  124.3 1.0 fusion.46
  125.4 3.2 fusion.45
  129.8 3.2 fusion.45
  134.2 3.2 fusion.45
  138.6 3.2 fusion.45
  143.0 3.2 fusion.45
  147.2 4.5 %reduce.16 = bf16[4096,256]{1,0:T(8,128)(2,1)} reduce(bf16[4096,1,256]{2,0,1:T(8,128)(2,1)} %bitcast.116, bf16[]{:T(256)} %broadcast.259), dimensions={1}, to_apply=%copy.68.reduce_sub_computation | reduce | bytes 4194306 | tf_op jit(solution)/shard_map/reshape | solution.py:41
  151.7 4.0 %reshape.319 = bf16[32,2,16384]{2,1,0:T(2,128)(2,1)} reshape(bf16[4096,256]{1,0:T(8,128)(2,1)} %reduce.16) | data formatting | bytes 4194304
  155.7 6.3 %all-to-all-done.1 = bf16[32,2,16384]{2,1,0:T(2,128)(2,1)S(1)} async-done(((bf16[32,2,16384]{2,1,0:T(2,128)(2,1)}), bf16[32,2,16384]{2,1,0:T(2,128)(2,1)S(1)}, u32[]{:S(2)}, u32[]{:S(2)}) %all-to-all-start.1) | async-done | bytes 2097184 | tf_op jit(solution)/shard_map/all_to_all | solution.py:96
  162.0 10.4 %all-to-all-start.2 = ((bf16[32,2,16384]{2,1,0:T(2,128)(2,1)}), bf16[32,2,16384]{2,1,0:T(2,128)(2,1)}, u32[]{:S(2)}, u32[]{:S(2)}) async-start(bf16[32,2,16384]{2,1,0:T(2,128)(2,1)} %reshape.319), calls=%async_computation.2 | async-start | bytes 4194304 | tf_op jit(solution)/shard_map/all_to_all | solution.py:96
  175.2 1.3 iota_compare_fusion.3
  177.5 6.7 %reshape.322 = bf16[4096,1,256]{2,1,0:T(2,128)(2,1)} reshape(bf16[32,2,16384]{2,1,0:T(2,128)(2,1)S(1)} %all-to-all-done.1) | data formatting | bytes 4194304
  184.2 2.5 copy.71
  186.8 41.1 %all-to-all-done.2 = bf16[32,2,16384]{2,1,0:T(2,128)(2,1)} async-done(((bf16[32,2,16384]{2,1,0:T(2,128)(2,1)}), bf16[32,2,16384]{2,1,0:T(2,128)(2,1)}, u32[]{:S(2)}, u32[]{:S(2)}) %all-to-all-start.2) | async-done | bytes 2097184 | tf_op jit(solution)/shard_map/all_to_all | solution.py:96
  227.9 10.4 %reshape.320 = bf16[4096,1,256]{2,1,0:T(2,128)(2,1)} reshape(bf16[32,2,16384]{2,1,0:T(2,128)(2,1)} %all-to-all-done.2) | data formatting | bytes 4194304
  238.3 2.6 copy.72
  241.3 2.4 copy.69
  243.7 6.2 %copy.77 = bf16[32,8,32,256]{3,1,2,0:T(8,128)(2,1)} copy(bf16[32,8,32,256]{3,2,1,0:T(8,128)(2,1)S(1)} %bitcast.114) | data formatting | bytes 8388608
  249.9 4.1 %convolution_convert_fusion.2 = bf16[256,128]{1,0:T(8,128)(2,1)S(1)} fusion(bf16[256,8192]{1,0:T(8,128)(2,1)} %bitcast.112, bf16[8192,128]{1,0:T(8,128)(2,1)} %all-gather.4.cloned.1.call-done), kind=kOutput, calls=%fused_computation.31 | convolution fusion | flops 536903680 | bytes 6356992 | tf_op jit(solution)/shard_map/dot_general | solution.py:101
  254.1 89.4 %all-gather.8.cloned.1.call-done = bf16[8192,1024]{1,0:T(8,128)(2,1)} async-done(((bf16[256,1024]{1,0:T(8,128)(2,1)}), bf16[8192,1024]{1,0:T(8,128)(2,1)}) %all-gather.8.cloned.1.call-update) | async-done | bytes 16777232 | tf_op jit(solution)/shard_map/all_gather | solution.py:118
  343.5 12.7 %fusion.17 = f32[256]{0:T(256)S(1)} fusion(bf16[8192,1024]{1,0:T(8,128)(2,1)} %all-gather.8.cloned.1.call-done, bf16[256,128]{1,0:T(8,128)(2,1)S(1)} %convolution_convert_fusion.2, bf16[128,8192]{1,0:T(8,128)(2,1)} %all-gather.6.cloned.1.call-done, bf16[256,8192]{1,0:T(8,128)(2,1)} %bitcast.113, f32[8192]{0:T(1024)S(1)} %copy-done.8, ...), kind=kOutput, calls=%fused_computation.30 | convolution fusion | flops 4843372544 | bytes 23176192 | tf_op jit(solution)/shard_map/dot_general | solution.py:116
  (107 shorter events, 26.2 us)
Async XLA Ops:
  7.2 166.8 %copy-start = (s32[1,4]{1,0:T(1,128)S(1)}, s32[1,4]{1,0:T(1,128)}, u32[]{:S(2)}) copy-start(s32[1,4]{1,0:T(1,128)} %param.20) | copy-start | bytes 52
  7.2 242.7 %all-gather.4.cloned.1.call-start = ((), (), s32[]{:S(2)}) async-start(), calls=%async_computation.3 | async-start | bytes 2162688 | tf_op jit(solution)/shard_map/all_gather | solution.py:103
  7.9 246.2 %all-gather.6.cloned.1.call-start = ((), (), s32[]{:S(2)}) async-start(), calls=%async_computation.4 | async-start | bytes 2162688 | tf_op jit(solution)/shard_map/all_gather | solution.py:109
  8.7 11.9 %copy-start.5 = (s32[2,4096,1,8]{1,3,2,0:T(8,128)S(1)}, s32[2,4096,1,8]{1,3,2,0:T(8,128)}, u32[]{:S(2)}) copy-start(s32[2,4096,1,8]{1,3,2,0:T(8,128)} %param.23) | copy-start | bytes 786436
  8.7 334.8 %all-gather.8.cloned.1.call-start = ((), (), s32[]{:S(2)}) async-start(), calls=%async_computation.5 | async-start | bytes 17301504 | tf_op jit(solution)/shard_map/all_gather | solution.py:118
  12.0 8.5 %copy-start.6 = (s32[2,1,4096]{2,1,0:T(1,128)S(1)}, s32[2,1,4096]{2,1,0:T(1,128)}, u32[]{:S(2)}) copy-start(s32[2,1,4096]{2,1,0:T(1,128)} %param.24) | copy-start | bytes 98308
  13.9 43.2 %all-to-all-start = ((bf16[8,1,2,128,256]{4,3,2,1,0:T(8,128)(2,1)}), bf16[8,1,2,128,256]{4,3,2,1,0:T(8,128)(2,1)S(1)}, u32[]{:S(2)}, u32[]{:S(2)}) async-start(bf16[8,1,2,128,256]{4,3,2,1,0:T(8,128)(2,1)} %broadcast_in_dim.137), calls=%async_computation | async-start | bytes 2097152 | tf_op jit(solution)/shard_map/all_to_all | solution.py:9
  52.9 2.2 copy-start.7
  52.9 4.4 %copy-start.3 = (bf16[1,4,128,256]{3,2,1,0:T(8,128)(2,1)S(1)}, bf16[1,4,128,256]{3,2,1,0:T(8,128)(2,1)}, u32[]{:S(2)}) copy-start(bf16[1,4,128,256]{3,2,1,0:T(8,128)(2,1)} %param.18) | copy-start | bytes 786436
  100.3 61.7 %all-to-all-start.1 = ((bf16[32,2,16384]{2,1,0:T(2,128)(2,1)}), bf16[32,2,16384]{2,1,0:T(2,128)(2,1)S(1)}, u32[]{:S(2)}, u32[]{:S(2)}) async-start(bf16[32,2,16384]{2,1,0:T(2,128)(2,1)} %reshape.321), calls=%async_computation.1 | async-start | bytes 4194304 | tf_op jit(solution)/shard_map/all_to_all | solution.py:96
  147.2 4.5 %copy-start.4 = (bf16[1,512,256]{2,1,0:T(8,128)(2,1)}, bf16[1,512,256]{2,1,0:T(8,128)(2,1)S(1)}, u32[]{:S(2)}) copy-start(bf16[1,512,256]{2,1,0:T(8,128)(2,1)S(1)} %get-tuple-element.330) | copy-start | bytes 786436
  155.7 20.8 %copy-start.2 = (bf16[1,8,128,256]{3,2,1,0:T(8,128)(2,1)S(1)}, bf16[1,8,128,256]{3,2,1,0:T(8,128)(2,1)}, u32[]{:S(2)}) copy-start(bf16[1,8,128,256]{3,2,1,0:T(8,128)(2,1)} %param.19) | copy-start | bytes 1572868
  162.0 65.9 %all-to-all-start.2 = ((bf16[32,2,16384]{2,1,0:T(2,128)(2,1)}), bf16[32,2,16384]{2,1,0:T(2,128)(2,1)}, u32[]{:S(2)}, u32[]{:S(2)}) async-start(bf16[32,2,16384]{2,1,0:T(2,128)(2,1)} %reshape.319), calls=%async_computation.2 | async-start | bytes 4194304 | tf_op jit(solution)/shard_map/all_to_all | solution.py:96
  249.9 93.6 %copy-start.8 = (f32[8192]{0:T(1024)S(1)}, f32[8192]{0:T(1024)}, u32[]{:S(2)}) copy-start(f32[8192]{0:T(1024)} %param.27) | copy-start | bytes 98308
  249.9 93.6 %copy-start.9 = (f32[1024]{0:T(1024)S(1)}, f32[1024]{0:T(1024)}, u32[]{:S(2)}) copy-start(f32[1024]{0:T(1024)} %param.30) | copy-start | bytes 12292
  249.9 93.6 %copy-start.10 = (f32[1024]{0:T(1024)S(1)}, f32[1024]{0:T(1024)}, u32[]{:S(2)}) copy-start(f32[1024]{0:T(1024)} %param.29) | copy-start | bytes 12292
  343.5 13.2 %copy-start.1 = (s32[1,4]{1,0:T(1,128)S(1)}, s32[1,4]{1,0:T(1,128)}, u32[]{:S(2)}) copy-start(s32[1,4]{1,0:T(1,128)} %param.20) | copy-start | bytes 52
Sparse Core Ops, SparseCore 0:
  10.6 77.0 all-gather.3
  90.1 95.1 all-gather.5
  187.9 155.6 all-gather.7
where the time goes:
time: 365 us; the launch traced here: 363 us
  waiting for transfers between devices  139 us (38%)
  local copies, waits for them, and re-layouts  88.8 us (24%)
  other arithmetic  65.7 us (18%)
  starting transfers between devices  27.5 us (8%)
  matrix products  27.3 us (7%)
  between operations  14.7 us (4%)
    all_gather x1, waiting for transfers between devices, on_device(): lax.all_gather(mlp_in, 'cache', axis=0, tiled=True)  89.4 us
    reduce_sum x16, other arithmetic, one_block(): jnp.sum((lookup_block[..., None] == codes).astype(jnp.bfloat16), axis=2)  51.7 us
    all_to_all x2, waiting for transfers between devices, on_device(): lax.all_to_all(pooled, 'cache', split_axis=0, concat_axis=1, tiled=True)  47.4 us
    unnamed x35, local copies, waits for them, and re-layouts  42.9 us
    gather x2, local copies, waits for them, and re-layouts, pool_batch(): requests = requests[order]  28.2 us
    all_to_all x2, starting transfers between devices, on_device(): lax.all_to_all(pooled, 'cache', split_axis=0, concat_axis=1, tiled=True)  20.7 us
    dot_general x1, matrix products, on_device(): jnp.dot(columns, lax.all_gather(mlp_in, 'cache', axis=0, tiled=True), pre...  12.7 us
    dot_general x16, matrix products, one_block(): jnp.einsum('rfk,fke->rfe', counts, table, preferred_element_type=jnp.floa...  10.5 us
  transfers between devices with their start and end apart: 6, of which 3 were waited for; matrix products, arithmetic and copies ran while one was open for 46% of the time, Pallas kernels for 0%

commit v1 on v0

--- a/solution.py
+++ b/solution.py
@@ -115,7 +115,9 @@
     columns = crossed
     before = jnp.dot(
         columns,
-        lax.all_gather(mlp_in, "cache", axis=0, tiled=True),
+        jnp.concatenate(
+            lax.all_to_all(jnp.stack([mlp_in] * lax.axis_size("cache")), "cache", 0, 0), axis=0
+        ),
         preferred_element_type=jnp.float32,
     )
     hidden = jnp.maximum(before + mlp_bias, 0.0)

time: 365 us -> 675 us (1.85)
  the two profiles are of different devices: /device:TPU:1 before, /device:TPU:163 now
where the time goes in v1:
time: 675 us; the launch traced here: 674 us
  waiting for transfers between devices  393 us (58%)
  local copies, waits for them, and re-layouts  93.1 us (14%)
  other arithmetic  65.8 us (10%)
  blocking collectives  56.7 us (8%)
  matrix products  27.3 us (4%)
  starting transfers between devices  22.8 us (3%)
  between operations  14.9 us (2%)
    all_gather x1, waiting for transfers between devices, on_device(): lax.all_gather(dcn_up, 'cache', axis=1, tiled=True)  300 us
    all_gather x1, waiting for transfers between devices, on_device(): lax.all_gather(dcn_down, 'cache', axis=0, tiled=True)  69.9 us
    all_to_all x1, blocking collectives, on_device(): lax.all_to_all(pooled, 'cache', split_axis=0, concat_axis=1, tiled=True)  56.7 us
    reduce_sum x16, other arithmetic, one_block(): jnp.sum((lookup_block[..., None] == codes).astype(jnp.bfloat16), axis=2)  51.7 us
    unnamed x39, local copies, waits for them, and re-layouts  41.3 us
    gather x2, local copies, waits for them, and re-layouts, pool_batch(): requests = requests[order]  28.4 us
    all_to_all x1, waiting for transfers between devices, on_device(): lax.all_to_all(jnp.stack([mlp_in] * lax.axis_size('cache')), 'cache', 0, 0)  19.1 us
  transfers between devices with their start and end apart: 5, of which 4 were waited for; matrix products, arithmetic and copies ran while one was open for 18% of the time, Pallas kernels for 0%

profile of v1, /device:TPU:163, one launch (start us, length us, event | category | flops | bytes accessed | tf_op | source)
XLA Modules:
  0.0 674.0 jit_solution(6672117433344591302)
XLA Ops:
  8.9 1.6 gather_fusion.2
  10.6 1.1 broadcast_in_dim.137
  11.7 5.1 all-to-all-start
  17.5 14.2 %gather_fusion.1 = s32[4096,8]{1,0:T(8,128)} fusion(s32[4096,8]{1,0:T(8,128)S(1)} %bitcast.112, s32[4096]{0:T(1024)S(1)} %broadcast_clamp_fusion), kind=kCustom, calls=%fused_computation.1 | custom fusion | bytes 278528 | tf_op jit(solution)/shard_map/gather | solution.py:28
  31.7 2.8 copy.67
  35.2 14.2 %gather_fusion = s32[4096,8]{1,0:T(8,128)} fusion(s32[4096,8]{1,0:T(8,128)S(1)} %bitcast.111, s32[4096]{0:T(1024)S(1)} %broadcast_clamp_fusion.1), kind=kCustom, calls=%fused_computation | custom fusion | bytes 278528 | tf_op jit(solution)/shard_map/gather | solution.py:28
  49.3 2.2 copy.64
  52.1 1.3 iota_compare_fusion.5
  53.9 35.3 %while.27 = (s32[]{:T(128)}, bf16[8,512,1,256]{3,1,2,0:T(8,128)(2,1)S(1)}, s32[8,512,1,8]{1,3,2,0:T(8,128)}, bf16[1,512,256]{2,1,0:T(8,128)(2,1)S(1)}, s32[]{:T(128)}) while((s32[]{:T(128)}, bf16[8,512,1,256]{3,1,2,0:T(8,128)(2,1)S(1)}, s32[8,512,1,8]{1,3,2,0:T(8,128)}, bf16[1,512,256]{2,1,0:T(8,128)(2,1)S(1)}, s32[]{:T(128)}) %tuple.88), condition=%wide.region_6.7_spmd.clone, body=%wide.region_4.6_spmd.clone.sunk | while | flops 140378112 | bytes 1654861 | solution.py:40
  54.8 3.2 fusion.45
  59.2 3.2 fusion.45
  63.6 3.2 fusion.45
  68.0 3.2 fusion.45
  72.5 3.2 fusion.45
  76.9 3.2 fusion.45
  81.3 3.2 fusion.45
  85.7 3.2 fusion.45
  89.8 2.9 reduce.16
  92.7 4.0 reshape.325
  96.7 8.8 %all-to-all-start.2 = ((bf16[32,2,16384]{2,1,0:T(2,128)(2,1)}), bf16[32,2,16384]{2,1,0:T(2,128)(2,1)S(1)}, u32[]{:S(2)}, u32[]{:S(2)}) async-start(bf16[32,2,16384]{2,1,0:T(2,128)(2,1)} %reshape.325), calls=%async_computation.2 | async-start | bytes 4194304 | tf_op jit(solution)/shard_map/all_to_all | solution.py:96
  105.5 1.5 broadcast.189.clone.1
  106.9 35.1 %while.26 = (s32[]{:T(128)}, bf16[8,512,1,256]{3,1,2,0:T(8,128)(2,1)}, s32[8,512,1,8]{1,3,2,0:T(8,128)S(1)}, bf16[1,512,256]{2,1,0:T(8,128)(2,1)S(1)}, s32[]{:T(128)}) while((s32[]{:T(128)}, bf16[8,512,1,256]{3,1,2,0:T(8,128)(2,1)}, s32[8,512,1,8]{1,3,2,0:T(8,128)S(1)}, bf16[1,512,256]{2,1,0:T(8,128)(2,1)S(1)}, s32[]{:T(128)}) %tuple.89), condition=%wide.region_3.4_spmd.clone, body=%wide.region_1.3_spmd.clone.sunk | while | flops 140378112 | bytes 1654861 | solution.py:40
  107.1 3.2 fusion.41
  111.4 3.2 fusion.41
  115.8 3.2 fusion.41
  120.2 3.2 fusion.41
  124.6 3.2 fusion.41
  129.0 3.2 fusion.41
  133.4 3.2 fusion.41
  137.8 3.2 fusion.41
  142.0 4.5 reduce.17
  146.5 4.0 reshape.327
  150.5 2.4 all-to-all-done.2
  152.9 56.7 %all_to_all.40 = bf16[32,2,16384]{2,1,0:T(2,128)(2,1)} all-to-all(bf16[32,2,16384]{2,1,0:T(2,128)(2,1)} %reshape.327), channel_id=1, replica_groups=mesh['cache'=32,'owner'=8] {'cache'}, dimensions={0} | all-to-all | bytes 4194304 | tf_op jit(solution)/shard_map/all_to_all | solution.py:96
  209.6 5.9 stack.11
  215.6 8.6 %all-to-all-start.3 = ((bf16[32,256,1024]{2,1,0:T(8,128)(2,1)}), bf16[32,256,1024]{2,1,0:T(8,128)(2,1)}, u32[]{:S(2)}, u32[]{:S(2)}) async-start(bf16[32,256,1024]{2,1,0:T(8,128)(2,1)} %stack.11), calls=%async_computation.3 | async-start | bytes 33554432 | tf_op jit(solution)/shard_map/all_to_all | solution.py:119
  228.5 1.3 iota_compare_fusion.3
  230.7 6.8 %reshape.326 = bf16[4096,1,256]{2,1,0:T(2,128)(2,1)} reshape(bf16[32,2,16384]{2,1,0:T(2,128)(2,1)S(1)} %all-to-all-done.2) | data formatting | bytes 4194304
  237.6 4.0 copy.72
  241.6 6.8 %reshape.328 = bf16[4096,1,256]{2,1,0:T(2,128)(2,1)} reshape(bf16[32,2,16384]{2,1,0:T(2,128)(2,1)S(1)} %copy-done.1) | data formatting | bytes 4194304
  248.4 2.7 copy.71
  251.7 2.4 copy.69
  254.1 6.4 copy.77
  260.4 69.9 %all-gather.3.cloned.1.call-done = bf16[8192,128]{1,0:T(8,128)(2,1)} async-done(((bf16[256,128]{1,0:T(8,128)(2,1)}), bf16[8192,128]{1,0:T(8,128)(2,1)}) %all-gather.3.cloned.1.call-update) | async-done | bytes 2097168 | tf_op jit(solution)/shard_map/all_gather | solution.py:103
  330.3 4.1 convolution_convert_fusion.2
  334.5 300.4 %all-gather.5.cloned.1.call-done = bf16[128,8192]{1,0:T(8,128)(2,1)} async-done(((bf16[128,256]{1,0:T(8,128)(2,1)}), bf16[128,8192]{1,0:T(8,128)(2,1)}) %all-gather.5.cloned.1.call-update) | async-done | bytes 2097168 | tf_op jit(solution)/shard_map/all_gather | solution.py:109
  634.9 19.1 %all-to-all-done.3 = bf16[32,256,1024]{2,1,0:T(8,128)(2,1)} async-done(((bf16[32,256,1024]{2,1,0:T(8,128)(2,1)}), bf16[32,256,1024]{2,1,0:T(8,128)(2,1)}, u32[]{:S(2)}, u32[]{:S(2)}) %all-to-all-start.3) | async-done | bytes 16777248 | tf_op jit(solution)/shard_map/all_to_all | solution.py:119
  653.9 12.7 %fusion.17 = f32[256]{0:T(256)S(1)} fusion(bf16[8192,1024]{1,0:T(8,128)(2,1)} %bitcast.24, bf16[256,128]{1,0:T(8,128)(2,1)S(1)} %convolution_convert_fusion.2, bf16[128,8192]{1,0:T(8,128)(2,1)} %all-gather.5.cloned.1.call-done, bf16[256,8192]{1,0:T(8,128)(2,1)} %bitcast.114, f32[8192]{0:T(1024)S(1)} %copy-done.10, f32[1024]{0:T(1024)S(1)} %copy-done.11, ...), kind=kOutput, calls=%fused_computation.30 | convolution fusion | flops 4843372544 | bytes 23176192 | tf_op jit(solution)/shard_map/dot_general | solution.py:116
  (110 shorter events, 28.6 us)
Async XLA Ops:
  7.2 220.1 %copy-start = (s32[1,4]{1,0:T(1,128)S(1)}, s32[1,4]{1,0:T(1,128)}, u32[]{:S(2)}) copy-start(s32[1,4]{1,0:T(1,128)} %param.20) | copy-start | bytes 52
  7.2 9.7 %copy-start.7 = (s32[2,4096,1,8]{1,3,2,0:T(8,128)S(1)}, s32[2,4096,1,8]{1,3,2,0:T(8,128)}, u32[]{:S(2)}) copy-start(s32[2,4096,1,8]{1,3,2,0:T(8,128)} %param.23) | copy-start | bytes 786436
  10.5 6.3 copy-start.8
  11.7 41.7 %all-to-all-start = ((bf16[8,1,2,128,256]{4,3,2,1,0:T(8,128)(2,1)}), bf16[8,1,2,128,256]{4,3,2,1,0:T(8,128)(2,1)S(1)}, u32[]{:S(2)}, u32[]{:S(2)}) async-start(bf16[8,1,2,128,256]{4,3,2,1,0:T(8,128)(2,1)} %broadcast_in_dim.137), calls=%async_computation | async-start | bytes 2097152 | tf_op jit(solution)/shard_map/all_to_all | solution.py:9
  49.3 2.2 copy-start.9
  49.3 4.3 copy-start.4
  96.7 56.2 %all-to-all-start.2 = ((bf16[32,2,16384]{2,1,0:T(2,128)(2,1)}), bf16[32,2,16384]{2,1,0:T(2,128)(2,1)S(1)}, u32[]{:S(2)}, u32[]{:S(2)}) async-start(bf16[32,2,16384]{2,1,0:T(2,128)(2,1)} %reshape.325), calls=%async_computation.2 | async-start | bytes 4194304 | tf_op jit(solution)/shard_map/all_to_all | solution.py:96
  142.0 4.5 copy-start.6
  150.5 59.1 %copy-start.5 = (bf16[256,1024]{1,0:T(8,128)(2,1)S(1)}, bf16[256,1024]{1,0:T(8,128)(2,1)}, u32[]{:S(2)}) copy-start(bf16[256,1024]{1,0:T(8,128)(2,1)} %param.28) | copy-start | bytes 1572868
  215.6 14.2 %copy-start.3 = (bf16[1,8,128,256]{3,2,1,0:T(8,128)(2,1)S(1)}, bf16[1,8,128,256]{3,2,1,0:T(8,128)(2,1)}, u32[]{:S(2)}) copy-start(bf16[1,8,128,256]{3,2,1,0:T(8,128)(2,1)} %param.19) | copy-start | bytes 1572868
  215.6 438.3 %all-to-all-start.3 = ((bf16[32,256,1024]{2,1,0:T(8,128)(2,1)}), bf16[32,256,1024]{2,1,0:T(8,128)(2,1)}, u32[]{:S(2)}, u32[]{:S(2)}) async-start(bf16[32,256,1024]{2,1,0:T(8,128)(2,1)} %stack.11), calls=%async_computation.3 | async-start | bytes 33554432 | tf_op jit(solution)/shard_map/all_to_all | solution.py:119
  224.2 106.2 %all-gather.3.cloned.1.call-start = ((), (), s32[]{:S(2)}) async-start(), calls=%async_computation.4 | async-start | bytes 2162688 | tf_op jit(solution)/shard_map/all_gather | solution.py:103
  224.9 410.0 %all-gather.5.cloned.1.call-start = ((), (), s32[]{:S(2)}) async-start(), calls=%async_computation.5 | async-start | bytes 2162688 | tf_op jit(solution)/shard_map/all_gather | solution.py:109
  237.6 4.0 copy-start.1
  248.4 2.9 copy-start.2
  330.3 323.6 %copy-start.10 = (f32[8192]{0:T(1024)S(1)}, f32[8192]{0:T(1024)}, u32[]{:S(2)}) copy-start(f32[8192]{0:T(1024)} %param.27) | copy-start | bytes 98308
  330.3 323.6 %copy-start.11 = (f32[1024]{0:T(1024)S(1)}, f32[1024]{0:T(1024)}, u32[]{:S(2)}) copy-start(f32[1024]{0:T(1024)} %param.30) | copy-start | bytes 12292
  330.3 323.6 %copy-start.12 = (f32[1024]{0:T(1024)S(1)}, f32[1024]{0:T(1024)}, u32[]{:S(2)}) copy-start(f32[1024]{0:T(1024)} %param.29) | copy-start | bytes 12292
Sparse Core Ops, SparseCore 0:
  227.6 102.7 all-gather.2
  332.8 302.0 all-gather.4
